TPU v7x, 256 devices: a whole 4x4x8 slice. The times are simulated.
256 devices in a mesh: gx: 8 (over z), gy: 4 (over y), gz: 8 (over x, core).
Axes of the slice: x: 4, y: 4, z: 8, core: 2. Of those that a mesh axis runs over, the one named last changes fastest.
Arguments:
- point_data: float32 [1, 6, 131072], P(None, None, ('gx', 'gy', 'gz')), may hold values from -1 to 1
- neighbours: int32 [1, 64, 64, 64, 32], P(None, 'gx', 'gy', 'gz'), may hold values from 0 to 131071, as said below
- counts: int32 [1, 64, 64, 64], P(None, 'gx', 'gy', 'gz'), may hold values from 1 to 32, as said below
- kernel_in: bfloat16 [6, 80], replicated, may hold values from -2.5 to 2.5
- kernel_mid: bfloat16 [80, 80], replicated, may hold values from -0.625 to 0.625
- kernel_out: bfloat16 [80, 64], replicated, may hold values from -0.625 to 0.625
- spectral: bfloat16 [2, 16, 16, 16, 64, 64], P(None, 'gz', 'gx', 'gy'), may hold values from -48 to 48
- skip_weight: bfloat16 [64, 64], replicated, may hold values from -0.75 to 0.75
Outputs:
- latent_out: float32 [1, 64, 64, 64, 64], P(None, 'gx', 'gy', 'gz')
Inputs may be any that keep to these rules, and one draw needn't show every extreme that they name: `neighbours`: points are owned by location: point j of a geometry belongs to the device at position j // 512 in the order gx, gy, gz. Every neighbour of a node is owned by the node's own device or by a device whose gx, gy and gz indices each differ from it by at most one. Slots s >= counts of the node are padding that names some point all the same. `counts`: on every device some node of every geometry has all 32 slots valid.
All inputs are finite; a program needn't handle non-finite values.
Results may differ from a plain program's by a relative error of at most 0.02.
Values may be sent and summed in bfloat16 or wider, within the bound.
A program may use at most 64 MiB of HBM per device.

v0:
```python
import functools
import math

import jax
import jax.numpy as jnp
import ml_dtypes
import numpy as np
from jax import lax
from jax.experimental import pallas as pl
from jax.experimental.pallas import tpu as pltpu
from jax.sharding import PartitionSpec as P

GRID = 64
MODES = 16
NB = 32
NORM_FLOOR = 1.0
GX, GY, GZ = 8, 4, 8
F32 = jnp.float32
BF16 = jnp.bfloat16
MESH = pl.DeviceIdType.MESH


def gelu(v):
    inner = v * (0.7978845608028654 + 0.035677408136300125 * (v * v))
    half = 0.5 * v
    return half + half * jnp.tanh(inner)


def twice_gelu(v):
    if not GELU16:
        return v + v * jnp.tanh(v * (0.7978845608028654 + 0.035677408136300125 * (v * v)))
    v = v.astype(BF16)
    inner = v * (BF16(0.7978845608028654) + BF16(0.035677408136300125) * (v * v))
    return v + v * jnp.tanh(inner)


SLOTS = 4
ROWS = 176
FOUR, SIX = 108, 162
GELU16 = True
OFFSETS = [(dx, dy, dz) for dx in (-1, 0, 1) for dy in (-1, 0, 1) for dz in (-1, 0, 1)]


def regroup():
    row = lax.broadcasted_iota(jnp.int32, (512, 512), 0)
    column = lax.broadcasted_iota(jnp.int32, (512, 512), 1)
    wanted = ((row >> 1) & 7) * 64 + (row >> 4) * 2 + (row & 1)
    return jnp.where(wanted == column, 1.0, 0.0).astype(BF16)


def halo_kernel(
    points_ref, near_ref, counts_ref, table_ref, slots_ref, blocks_ref, info_ref, rank_ref,
    main, send, recv,
):
    me_x = lax.axis_index("gx")
    me_y = lax.axis_index("gy")
    me_z = lax.axis_index("gz")

    def device(offset):
        dx, dy, dz = offset
        return {
            "gx": lax.rem(me_x + dx + GX, GX),
            "gy": lax.rem(me_y + dy + GY, GY),
            "gz": lax.rem(me_z + dz + GZ, GZ),
        }

    barrier = pltpu.get_barrier_semaphore()
    peers = [o for o in OFFSETS if o != (0, 0, 0)]
    for offset in peers:
        pl.semaphore_signal(barrier, inc=1, device_id=device(offset), device_id_type=MESH)

    main[13] = jnp.concatenate([points_ref[d] for d in range(6)] + [jnp.zeros((2, 512), F32)], axis=0).astype(BF16)
    pl.semaphore_wait(barrier, len(peers))
    for offset in sorted(peers, key=lambda o: -sum(abs(d) for d in o)):
        slot = 26 - OFFSETS.index(offset)
        pltpu.make_async_remote_copy(
            src_ref=main.at[13],
            dst_ref=main.at[slot],
            send_sem=send.at[0],
            recv_sem=recv.at[0],
            device_id=device(offset),
            device_id_type=MESH,
        ).start()
    everything = main.at[pl.ds(0, 26)]

    lane = lax.broadcasted_iota(jnp.int32, (1, 1024), 1)
    counts = jnp.concatenate([counts_ref[x].astype(F32) for x in range(8)], axis=1)
    counts = jnp.concatenate([counts[z : z + 1] for z in range(8)], axis=1)
    key = counts * 1024.0 + (1023 - lane).astype(F32)
    ones = jnp.ones((8, 128), BF16)
    rank = jnp.zeros((8, 1024), F32)
    for m in range(8):
        tall = jnp.broadcast_to(key[:, 128 * m : 128 * m + 128], (128, 128)).T
        ahead = jnp.concatenate(
            [
                jnp.where(tall > key[:, 128 * n : 128 * n + 128], 1.0, 0.0).astype(BF16)
                for n in range(8)
            ],
            axis=1,
        )
        rank = rank + jnp.dot(ones, ahead, preferred_element_type=F32)
    rank_ref[...] = rank
    near = jnp.concatenate(
        [near_ref[pl.ds(z, 128, stride=8), :].astype(F32).T for z in range(8)], axis=1
    ).astype(jnp.int32)
    owner = near >> 9
    part = near & 511
    block = ((((owner >> 5) - me_x + 1) * 3) + ((owner >> 3) & 3) - me_y + 1) * 3 + (owner & 7) - me_z + 1
    code = jnp.clip(block, 0, 26) * 2 + (part >> 8)
    place_y = (me_y * 16 + (lane & 15)).astype(F32)
    place_x = (me_x * 8 + ((lane >> 4) & 7)).astype(F32)
    place_z = (me_z * 8 + (lane >> 7)).astype(F32)
    centres = [-(place + 0.5) / GRID for place in (place_x, place_y, place_z)]
    rows = jnp.concatenate(
        [(part & 255).astype(F32), code.astype(F32), counts] + centres + [jnp.zeros((12, 1024), F32)], axis=0
    ).astype(BF16)
    order = lax.broadcasted_iota(jnp.int32, (128, 1024), 0).astype(F32)
    wide_rank = rank[0:1]
    for t in range(8):
        moved = jnp.where(order + 128.0 * t == wide_rank, 1.0, 0.0).astype(BF16)
        moved = lax.dot_general(rows, moved, (((1,), (1,)), ((), ())), preferred_element_type=F32)
        slots_ref[t] = moved[0:32].astype(jnp.int32)
        blocks_ref[t] = moved[32:64].astype(jnp.int32)
        info_ref[t] = moved[64:72]

    pltpu.make_async_copy(everything, everything, recv.at[0]).wait()
    blocks = [main[b].astype(F32) for b in range(27)]
    rows = [block[0:4] for block in blocks] + [block[4:6] for block in blocks]
    rows.append(jnp.zeros((ROWS - SIX, 512), F32))
    rows = jnp.concatenate(rows, axis=0).astype(BF16)
    table_ref[0:ROWS, :] = rows[:, 0:256]
    table_ref[ROWS : 2 * ROWS, :] = rows[:, 256:512]
    pltpu.make_async_copy(everything, everything, send.at[0]).wait()


def halo(points, near, counts):
    vmem = pl.BlockSpec(memory_space=pltpu.VMEM)
    return pl.pallas_call(
        halo_kernel,
        out_shape=[
            jax.ShapeDtypeStruct((2 * ROWS, 256), BF16),
            jax.ShapeDtypeStruct((8, NB, 128), jnp.int32),
            jax.ShapeDtypeStruct((8, NB, 128), jnp.int32),
            jax.ShapeDtypeStruct((8, 8, 128), F32),
            jax.ShapeDtypeStruct((8, 1024), F32),
        ],
        in_specs=[vmem] * 3,
        out_specs=[vmem] * 5,
        scratch_shapes=[
            pltpu.VMEM((27, 8, 512), BF16),
            pltpu.SemaphoreType.DMA((1,)),
            pltpu.SemaphoreType.DMA((1,)),
        ],
        compiler_params=pltpu.CompilerParams(collective_id=1, has_side_effects=True),
    )(points, near, counts)


def encoder_kernel(
    table_ref, slots_ref, blocks_ref, info_ref, in_ref, mid_ref, last_ref, out_ref,
    first_scr, mid_scr, last_scr, kept_scr, hidden_scr, base_scr, totals, trips,
):
    column = lax.broadcasted_iota(jnp.int32, (6, ROWS), 1)
    feature = lax.broadcasted_iota(jnp.int32, (6, ROWS), 0)
    wanted = jnp.where(column < FOUR, column % 4, 4 + column % 2)
    wanted = jnp.where(column >= SIX, column - SIX, wanted)
    chosen = jnp.where((feature == wanted) & (column < SIX + 3), 1.0, 0.0).astype(BF16)
    turn = (((0,), (0,)), ((), ()))
    first_scr[...] = lax.dot_general(in_ref[...], chosen, turn, preferred_element_type=F32).astype(BF16)
    half_mid = (mid_ref[...].astype(F32).T * 0.5).astype(BF16)
    mid_scr[...] = jnp.zeros(mid_scr.shape, BF16)
    mid_scr[0:80, 0:80] = half_mid
    mid_scr[80:160, 80:160] = half_mid
    last_scr[...] = last_ref[...]

    slot_ids = lax.broadcasted_iota(jnp.int32, (256, 128), 0).astype(jnp.int16)
    row = lax.broadcasted_iota(jnp.int32, (ROWS, 128), 0)
    row_block = jnp.where(row < FOUR, row // 4, jnp.where(row < SIX, (row - FOUR) // 2, -1)).astype(jnp.int16)
    last_rows = lax.broadcasted_iota(jnp.int32, (16, 128), 0)
    steps = 0
    for c in range(8):
        info = info_ref[c]
        trip = (jnp.max(info[0:1]).astype(jnp.int32) + SLOTS - 1) // SLOTS
        trips[c] = trip
        steps += trip
        centre = jnp.zeros((16, 128), F32)
        for d in range(3):
            centre = jnp.where(last_rows == SIX - ROWS + 16 + d, info[1 + d : 2 + d], centre)
        base_scr[c] = centre.astype(BF16)
        totals[c] = jnp.zeros((80, 128), F32)
    totals[8] = jnp.zeros((80, 128), F32)
    kept_scr[...] = jnp.zeros(kept_scr.shape, BF16)
    hidden_scr[...] = jnp.zeros(hidden_scr.shape, BF16)

    def step(n, places):
        (c0, t0), (c1, t1), (c2, t2) = places
        hidden = twice_gelu(jnp.dot(mid_scr[...], hidden_scr[...], preferred_element_type=F32))
        counts = info_ref[jnp.minimum(c2, 7), 0:1, :]
        total = totals[c2]
        for u in range(SLOTS):
            used = (SLOTS * t2 + u).astype(F32) < counts
            here = hidden[80 * (u // 2) : 80 * (u // 2) + 80, 128 * (u % 2) : 128 * (u % 2) + 128]
            total = total + jnp.where(used, here.astype(F32), 0.0)
        totals[c2] = total
        hidden = jnp.dot(first_scr[...], kept_scr[...], preferred_element_type=F32)
        hidden = twice_gelu(hidden).astype(BF16)
        for u in range(SLOTS // 2):
            hidden_scr[80 * u : 80 * u + 80, :] = hidden[:, 256 * u : 256 * u + 256]
        hot = []
        for u in range(SLOTS):
            slot = jnp.broadcast_to(slots_ref[c0, pl.ds(SLOTS * t0 + u, 1), :], (16, 128)).astype(jnp.int16)
            slot = jnp.concatenate([slot] * 16, axis=0)
            hot.append(jnp.where(slot_ids == slot, BF16(1), BF16(0)))
        found = jnp.dot(table_ref[...], jnp.concatenate(hot, axis=1), preferred_element_type=F32)
        found = found.astype(BF16)
        for u in range(SLOTS):
            code = jnp.broadcast_to(blocks_ref[c0, pl.ds(SLOTS * t0 + u, 1), :], (16, 128))
            block = (code >> 1).astype(jnp.int16)
            odd = (code & 1).astype(jnp.int16)
            same = row_block == jnp.concatenate([block] * (ROWS // 16), axis=0)
            odd = jnp.concatenate([odd] * (ROWS // 16), axis=0) == 1
            here = found[:, 128 * u : 128 * u + 128]
            here = jnp.where(odd, here[ROWS : 2 * ROWS], here[0:ROWS])
            kept_scr[0 : ROWS - 16, 128 * u : 128 * u + 128] = jnp.where(same[0 : ROWS - 16], here[0 : ROWS - 16], BF16(0))
            kept_scr[ROWS - 16 : ROWS, 128 * u : 128 * u + 128] = jnp.where(same[ROWS - 16 : ROWS], here[ROWS - 16 : ROWS], base_scr[c0])
        ended = t0 + 1 >= trips[c0]
        following = (
            jnp.minimum(jnp.where(ended, c0 + 1, c0), 7),
            jnp.where(ended, jnp.where(c0 == 7, t0, 0), t0 + 1),
        )
        return following, (c0, t0), (c1, t1)

    start = (jnp.int32(0), jnp.int32(0))
    spare = (jnp.int32(8), jnp.int32(0))
    lax.fori_loop(0, steps + 2, step, (start, spare, spare))
    last = last_scr[...]
    ordered = []
    for c in range(8):
        mean = totals[c] * (0.5 / info_ref[c, 0:1, :])
        upper = mean.astype(BF16)
        lower = (mean - upper.astype(F32)).astype(BF16)
        values = jnp.dot(last, upper, preferred_element_type=F32) + jnp.dot(
            last, lower, preferred_element_type=F32
        )
        ordered.append(values.astype(BF16))
    out_ref[...] = jnp.concatenate(ordered, axis=1)


def encode(table, slots, blocks, info, kernel_in, kernel_mid, kernel_out):
    vmem = pl.BlockSpec(memory_space=pltpu.VMEM)
    return pl.pallas_call(
        encoder_kernel,
        out_shape=jax.ShapeDtypeStruct((64, 1024), BF16),
        in_specs=[vmem] * 7,
        out_specs=vmem,
        scratch_shapes=[
            pltpu.VMEM((80, ROWS), BF16),
            pltpu.VMEM((160, 160), BF16),
            pltpu.VMEM((64, 80), BF16),
            pltpu.VMEM((ROWS, 128 * SLOTS), BF16),
            pltpu.VMEM((160, 256), BF16),
            pltpu.VMEM((8, 16, 128), BF16),
            pltpu.VMEM((9, 80, 128), F32),
            pltpu.SMEM((8,), jnp.int32),
        ],
    )(table, slots, blocks, info, kernel_in, kernel_mid, kernel_out)


def halves(values):
    upper = values.astype(np.float32).astype(ml_dtypes.bfloat16)
    lower = (values - upper.astype(np.float64)).astype(np.float32).astype(ml_dtypes.bfloat16)
    return np.stack([upper, lower])


def turn(frequency, position):
    angle = 2.0 * math.pi * ((frequency * position) % GRID) / GRID
    return np.cos(angle), np.sin(angle)


def centred(index):
    return np.where(index < MODES // 2, index, index - MODES)


def complex_block(cos, sin):
    return np.stack([np.stack([cos, sin], -1), np.stack([-sin, cos], -1)], -2)


@functools.lru_cache(None)
def third_table():
    cos, sin = turn(np.arange(16)[:, None], np.arange(64)[None, :])
    parts = np.stack([cos, -sin]).reshape(2, 16, 8, 8)
    full = np.einsum("akgz,cd->akcgdz", parts, np.eye(2))
    return full.reshape(64, 128)


@functools.lru_cache(None)
def second_table():
    j = np.arange(16)
    cos, sin = turn(centred(j)[:, None], np.arange(64)[None, :])
    both = complex_block(cos, sin).reshape(8, 2, 4, 16, 2, 2)
    full = np.einsum("gleyab,xw->lgaxebwy", both, np.eye(8))
    return full.reshape(2, 128, 1024)


@functools.lru_cache(None)
def first_table():
    i = np.arange(16)
    cos, sin = turn(centred(i)[:, None], np.arange(64)[None, :])
    both = complex_block(cos, sin).reshape(8, 2, 8, 8, 2, 2)
    return np.einsum("hltxab->tlhabx", both).reshape(8, 2, 16, 16)


def placed(values):
    return np.tile(np.moveaxis(halves(values), 0, 1), (1, 1, 1, 1, 8))


@functools.lru_cache(None)
def pair_table():
    out = np.zeros((4, 8, 8, 2, 8, 8, 2))
    for il in range(2):
        for jl in range(2):
            for h in range(8):
                for g in range(8):
                    i, j = 2 * h + il, 2 * g + jl
                    if i == 8 or j == 8:
                        continue
                    ni, nj = (16 - i) % 16, (16 - j) % 16
                    assert ni % 2 == il and nj % 2 == jl
                    for a in range(2):
                        out[2 * il + jl, g, h, a, nj // 2, ni // 2, a] = 1.0 - 2.0 * a
    return out.reshape(4, 128, 128)


def dotf(a, b):
    return jnp.dot(a, b, preferred_element_type=F32)


def dott(a, b):
    return lax.dot_general(a, b, (((1,), (1,)), ((), ())), preferred_element_type=F32)


def split(values):
    upper = values.astype(BF16)
    return upper, (values - upper.astype(F32)).astype(BF16)


def spectral_kernel(
    ordered_ref, rank_ref, skip_ref, weight_any, third_any, back_any, second_any, first_any, firstt_any, pair_any,
    out_ref,
    weight_ref, third_ref, back_ref, second_ref, first_ref, firstt_ref, pair_ref,
    latent, l_msg, r1, w_msg, rw, s_msg, r3, mixing, mixed_scr, n_msg, r5, g_msg, r6, b_msg, r8, ended, skip,
    send, recv, loaded,
):
    me_x = lax.axis_index("gx")
    me_y = lax.axis_index("gy")
    me_z = lax.axis_index("gz")
    me_q = me_y * GZ + me_z
    columns = [(y, z) for y in range(GY) for z in range(GZ) if y or z]
    columns.sort(key=lambda o: -(2 * min(o[0], GY - o[0]) + min(o[1], GZ - o[1])))

    def across(o):
        y, z = lax.rem(me_y + o[0], GY), lax.rem(me_z + o[1], GZ)
        return {"gy": y, "gz": z}, y * GZ + z, me_q

    def along_x(o):
        peer = lax.rem(me_x + o, GX)
        return {"gx": peer}, peer, me_x

    planes = [across(o) for o in columns]
    lines = [along_x(o) for o in (4, 3, 5, 2, 6, 1, 7)]
    barrier = pltpu.get_barrier_semaphore()
    for device, _, _ in lines + planes:
        pl.semaphore_signal(barrier, inc=1, device_id=device, device_id_type=MESH)
    constants = (weight_any, third_any, back_any, second_any, first_any, firstt_any, pair_any)
    copies = (weight_ref, third_ref, back_ref, second_ref, first_ref, firstt_ref, pair_ref)
    loads = [pltpu.make_async_copy(c, d, loaded.at[n]) for n, (c, d) in enumerate(zip(constants, copies))]
    for load in loads:
        load.start()
    order = lax.broadcasted_iota(jnp.int32, (1024, 128), 0).astype(F32)
    for z in range(8):
        moved = jnp.where(order == rank_ref[0:1, 128 * z : 128 * z + 128], 1.0, 0.0).astype(BF16)
        latent[64 * z : 64 * z + 64] = dotf(ordered_ref[...], moved)
    for q in range(32):
        both = [latent[pl.ds(2 * q + c, 8, stride=64), :] for c in range(2)]
        l_msg[q] = jnp.concatenate(both, axis=0).astype(BF16)
    pl.semaphore_wait(barrier, len(planes + lines))

    sends = []

    def start(stage, peers, source, target):
        for device, peer, me in peers:
            pltpu.make_async_remote_copy(
                src_ref=source(peer),
                dst_ref=target.at[me],
                send_sem=send.at[stage],
                recv_sem=recv.at[stage],
                device_id=device,
                device_id_type=MESH,
            ).start()
        everything = target.at[pl.ds(0, len(peers))]
        sends.append((stage, everything))
        return stage, everything

    def finish(pending):
        stage, everything = pending
        pltpu.make_async_copy(everything, everything, recv.at[stage]).wait()

    rows128 = lax.broadcasted_iota(jnp.int32, (128, 128), 0)
    lanes128 = lax.broadcasted_iota(jnp.int32, (128, 128), 1)
    same = rows128 // 16 == lanes128 // 16

    def spread_blocks(ref, part, l):
        small = ref[me_x, part, l].astype(F32)
        return jnp.where(same, jnp.concatenate([small] * 8, axis=0), 0.0).astype(BF16)

    first = start(0, planes, lambda p: l_msg.at[p], r1)
    r1[me_q] = l_msg[me_q]
    loads[0].wait()
    forth = regroup()
    for l in range(2):
        wide = jnp.concatenate(
            [weight_ref[b, 8 * l : 8 * l + 8].astype(F32).reshape(512, 64) for b in range(2)], axis=1
        ).astype(BF16)
        w_msg[:, 16 * l : 16 * l + 16, :] = dotf(forth, wide).astype(BF16).reshape(32, 16, 128)
    weights = start(1, planes, lambda p: w_msg.at[p], rw)
    rw[me_q] = w_msg[me_q]
    for load in loads[1:]:
        load.wait()
    first_tab = [[spread_blocks(first_ref, p, l) for l in range(2)] for p in range(2)]
    back_tab = [[spread_blocks(firstt_ref, p, l) for l in range(2)] for p in range(2)]
    skip_t = skip_ref[...].astype(F32).T.astype(BF16)
    for z in range(8):
        skip[z] = dotf(skip_t, latent[64 * z : 64 * z + 64].astype(BF16))
    finish(first)

    pieces = []
    for e in range(4):
        values = r1[8 * e : 8 * e + 8].reshape(128, 128)
        piece = dotf(third_ref[0], values) + dotf(third_ref[1], values)
        pieces += [piece[0:32], piece[32:64]]
    wide = jnp.concatenate(pieces, axis=1).astype(BF16)
    rows = jnp.concatenate(
        [dott(second_ref[0, l], wide) + dott(second_ref[1, l], wide) for l in range(2)], axis=1
    )
    upper, lower = split(rows)
    partial = jnp.concatenate(
        [
            dotf(first_tab[0][l], upper) + dotf(first_tab[0][l], lower) + dotf(first_tab[1][l], upper)
            for l in range(2)
        ],
        axis=1,
    )
    s_msg[...] = partial.astype(BF16).reshape(8, 16, 128)

    third = start(2, lines, lambda p: s_msg.at[p], r3)
    r3[me_x] = s_msg[me_x]
    finish(weights)
    for h in range(8):
        parts = [
            rw[e * 8 + h, 8 * p : 8 * p + 8, :].astype(F32) for p in range(4) for e in range(4)
        ]
        mixing[h] = jnp.concatenate(parts, axis=0).T.astype(BF16)
    finish(third)
    modes = jnp.sum(r3[...].astype(F32), axis=0)

    own = rows128 // 2 == lanes128 // 2
    even = lax.broadcasted_iota(jnp.int32, (64, 128), 1) % 2 == 0
    products = []
    for h in range(8):
        expanded = jnp.concatenate(
            [
                jnp.where(own, jnp.broadcast_to(modes[2 * h + a : 2 * h + a + 1], (128, 128)), 0.0)
                for a in range(2)
            ],
            axis=0,
        ).astype(BF16)
        products.append(dott(mixing[h], expanded))
    for h, product in enumerate(products):
        mixed_scr[h, 0:64] = product[0:64, 0:128] - product[64:128, 128:256]
        mixed_scr[h, 64:128] = product[64:128, 0:128] + product[0:64, 128:256]
    turned = [
        jnp.where(even, mixed_scr[h, pl.ds(0, 64, stride=2), :], mixed_scr[h, pl.ds(1, 64, stride=2), :])
        for h in range(8)
    ]
    place = lax.broadcasted_iota(jnp.int32, (512, 512), 0)
    source = lax.broadcasted_iota(jnp.int32, (512, 512), 1)
    wanted = ((place >> 1) & 7) * 64 + (place & 1) * 32 + (place >> 4)
    order = jnp.where(wanted == source, 1.0, 0.0).astype(BF16)
    turned = jnp.concatenate(turned, axis=0).astype(BF16)
    n_msg[...] = dotf(order, turned).astype(BF16).reshape(32, 16, 128)

    fourth = start(3, planes, lambda p: n_msg.at[p], r5)
    r5[me_q] = n_msg[me_q]
    finish(fourth)
    mixed = jnp.sum(r5[...].astype(F32), axis=0)
    zero_rows = lax.broadcasted_iota(jnp.int32, (16, 128), 0)
    zero_lanes = lax.broadcasted_iota(jnp.int32, (16, 128), 1)
    mixed = jnp.where((zero_rows < 2) & (zero_lanes < 2) & (me_x == 0), 0.0, mixed)
    g_msg[...] = mixed.astype(BF16)

    fifth = start(4, lines, lambda p: g_msg, r6)
    r6[me_x] = g_msg[...]
    finish(fifth)
    field = r6[...].reshape(128, 128)
    along = (
        dotf(back_tab[0][0], field[:, 0:64])
        + dotf(back_tab[1][0], field[:, 0:64])
        + dotf(back_tab[0][1], field[:, 64:128])
        + dotf(back_tab[1][1], field[:, 64:128])
    )
    upper, lower = split(along.T)
    plane = (
        dotf(upper[0:32], second_ref[0, 0])
        + dotf(lower[0:32], second_ref[0, 0])
        + dotf(upper[0:32], second_ref[1, 0])
        + dotf(upper[32:64], second_ref[0, 1])
        + dotf(lower[32:64], second_ref[0, 1])
        + dotf(upper[32:64], second_ref[1, 1])
    )
    scale = 1.0 / GRID**3
    plane_rows = lax.broadcasted_iota(jnp.int32, (32, 1024), 0)
    plane = (plane * jnp.where(plane_rows < 2, scale, 2.0 * scale)).astype(BF16)
    wide_field = field.astype(F32)
    paired = jnp.zeros((128, 128), F32)
    for p in range(4):
        paired = jnp.where(lanes128 // 32 == p, dotf(pair_ref[p], field), paired)
    low = (lanes128 // 2) % 16 == 0
    power = jnp.where(low, 0.5 * wide_field * (wide_field + paired), 2.0 * wide_field * wide_field)
    power = jnp.sum(power, axis=0, keepdims=True)
    for shift in (64, 32, 16, 8, 4, 2):
        power = power + pltpu.roll(power, shift, 1)
    lane = lax.broadcasted_iota(jnp.int32, (1, 128), 1)
    power = jnp.where(lane % 2 == (lane // 8) % 2, power, pltpu.roll(power, 1, 1))
    variance = jnp.broadcast_to(power, (128, 128)).T * (scale * scale)
    inverse = 1.0 / jnp.sqrt(variance + NORM_FLOOR)
    for e in range(4):
        part = jnp.concatenate(
            [plane[:, (2 * e + b) * 128 : (2 * e + b + 1) * 128] for b in range(2)], axis=0
        )
        branch = (dotf(back_ref[0], part) + dotf(back_ref[1], part)) * inverse
        b_msg[8 * e : 8 * e + 8] = branch.astype(BF16).reshape(8, 16, 128)

    sixth = start(5, planes, lambda p: b_msg.at[p], r8)
    r8[me_q] = b_msg[me_q]
    finish(sixth)
    ended[...] = r8[...].reshape(512, 128).astype(F32)
    for z in range(8):
        out_ref[z] = ended[pl.ds(z, 64, stride=8), :] + skip[z]
    for stage, everything in sends:
        pltpu.make_async_copy(everything, everything, send.at[stage]).wait()


def final_kernel(cells_ref, out_ref):
    for z in range(8):
        out_ref[:, z, :] = gelu(cells_ref[z]).T


def final(cells):
    vmem = pl.BlockSpec(memory_space=pltpu.VMEM)
    return pl.pallas_call(
        final_kernel, out_shape=jax.ShapeDtypeStruct((128, 8, 64), F32), in_specs=[vmem], out_specs=vmem
    )(cells)


def spectral_layer(ordered, rank, skip_w, weight, *tables):
    vmem = pl.BlockSpec(memory_space=pltpu.VMEM)
    own = [pltpu.VMEM(array.shape, array.dtype) for array in (weight,) + tables]
    return pl.pallas_call(
        spectral_kernel,
        out_shape=jax.ShapeDtypeStruct((8, 64, 128), F32),
        in_specs=[vmem] * 3 + [pl.BlockSpec(memory_space=pl.ANY)] * 7,
        out_specs=vmem,
        scratch_shapes=own
        + [
            pltpu.VMEM((512, 128), F32),
            pltpu.VMEM((32, 16, 128), BF16),
            pltpu.VMEM((32, 16, 128), BF16),
            pltpu.VMEM((32, 32, 128), BF16),
            pltpu.VMEM((32, 32, 128), BF16),
            pltpu.VMEM((8, 16, 128), BF16),
            pltpu.VMEM((8, 16, 128), BF16),
            pltpu.VMEM((8, 128, 128), BF16),
            pltpu.VMEM((8, 128, 128), F32),
            pltpu.VMEM((32, 16, 128), BF16),
            pltpu.VMEM((32, 16, 128), BF16),
            pltpu.VMEM((16, 128), BF16),
            pltpu.VMEM((8, 16, 128), BF16),
            pltpu.VMEM((32, 16, 128), BF16),
            pltpu.VMEM((32, 16, 128), BF16),
            pltpu.VMEM((512, 128), F32),
            pltpu.VMEM((8, 64, 128), F32),
            pltpu.SemaphoreType.DMA((6,)),
            pltpu.SemaphoreType.DMA((6,)),
            pltpu.SemaphoreType.DMA((7,)),
        ],
        compiler_params=pltpu.CompilerParams(collective_id=0, has_side_effects=True),
    )(ordered, rank, skip_w, weight, *tables)


def body(point_data, neighbours, counts, kernel_in, kernel_mid, kernel_out, spectral, skip_weight):
    cells_x, cells_y, cells_z = neighbours.shape[1:4]
    made = halo(
        jnp.transpose(point_data, (1, 0, 2)),
        neighbours.reshape(-1, NB),
        jnp.transpose(counts[0], (0, 2, 1)),
    )
    ordered = encode(*made[:4], kernel_in, kernel_mid, kernel_out.T)
    third = third_table()
    by_place = first_table()
    cells = spectral_layer(
        ordered,
        made[4],
        skip_weight,
        spectral.reshape(2, 16, 64, 64),
        jnp.asarray(halves(third)),
        jnp.asarray(halves(third.T)),
        jnp.asarray(halves(second_table())),
        jnp.asarray(placed(by_place)),
        jnp.asarray(placed(np.swapaxes(by_place, 2, 3))),
        jnp.asarray(pair_table().astype(ml_dtypes.bfloat16)),
    )
    out = final(cells)
    return out.reshape(1, cells_x, cells_y, cells_z, -1)


def solution(mesh):
    in_specs = (
        P(None, None, ("gx", "gy", "gz")),
        P(None, "gx", "gy", "gz", None),
        P(None, "gx", "gy", "gz"),
        P(),
        P(),
        P(),
        P(None, "gz", "gx", "gy", None, None),
        P(),
    )
    out_specs = P(None, "gx", "gy", "gz", None)
    return jax.shard_map(body, mesh=mesh, in_specs=in_specs, out_specs=out_specs, check_vma=False)
```

profile of v0, /device:TPU:1, one launch (start us, length us, event | category | flops | bytes accessed | tf_op | source)
XLA Modules:
  0.0 66.9 jit_solution(7112045264394738578)
XLA Ops:
  0.0 16.1 %shard_map.136 = (bf16[352,256]{1,0:T(8,128)(2,1)}, s32[8,32,128]{2,1,0:T(8,128)}, s32[8,32,128]{2,1,0:T(8,128)}, f32[8,8,128]{2,1,0:T(8,128)}, f32[8,1024]{1,0:T(8,128)}) custom-call(f32[6,1,512]{2,1,0:T(1,128)} %bitcast.12, s32[1024,32]{1,0:T(8,128)} %bitcast.9, s32[8,8,16]{2,1,0:T(8,128)} %bitcast.10), custom_call_target="tpu_custom_call" | custom-call | tf_op jit(solution)/shard_map/pallas_call | solution.py:138
  16.1 14.0 %shard_map.137.ordered_ref = bf16[64,1024]{1,0:T(8,128)(2,1)} custom-call(bf16[352,256]{1,0:T(8,128)(2,1)} %get-tuple-element.10.table_ref, s32[8,32,128]{2,1,0:T(8,128)} %get-tuple-element.11.slots_ref, s32[8,32,128]{2,1,0:T(8,128)} %get-tuple-element.12.blocks_ref, f32[8,8,128]{2,1,0:T(8,128)} %get-tuple-element.13.info_ref, bf16[6,80]{1,0:T(8,128)(2,1)} %in_ref.1, ...), custom_call_target="tpu_custom_call" | custom-call | tf_op jit(solution)/shard_map/pallas_call | solution.py:250
  30.1 34.6 %shard_map.138.cells_ref = f32[8,64,128]{2,1,0:T(8,128)} custom-call(bf16[64,1024]{1,0:T(8,128)(2,1)} %shard_map.137.ordered_ref, f32[8,1024]{1,0:T(8,128)} %get-tuple-element.14.rank_ref, bf16[64,64]{1,0:T(8,128)(2,1)} %skip_ref.1, bf16[2,16,64,64]{3,2,1,0:T(8,128)(2,1)} %bitcast.8, bf16[2,64,128]{2,1,0:T(8,128)(2,1)} %constant.12.clone.third_any, ...), custom_call_target="tpu_custom_call" | custom-call | tf_op jit(solution)/shard_map/pallas_call | solution.py:567
  64.8 2.1 %shard_map.139 = f32[128,8,64]{2,1,0:T(8,128)} custom-call(f32[8,64,128]{2,1,0:T(8,128)} %shard_map.138.cells_ref), custom_call_target="tpu_custom_call" | custom-call | tf_op jit(solution)/shard_map/pallas_call | solution.py:559
where the time goes:
time: 66.9 us
  Pallas kernels  66.9 us (100%)
    pallas_call x1, Pallas kernels, spectral_layer(): pl.pallas_call(spectral_kernel, out_shape=jax.ShapeDtypeStruct((8, 64, 12...  34.6 us
    pallas_call x1, Pallas kernels, halo(): pl.pallas_call(halo_kernel, out_shape=[jax.ShapeDtypeStruct((2 * ROWS, 25...  16.1 us
    pallas_call x1, Pallas kernels, encode(): pl.pallas_call(encoder_kernel, out_shape=jax.ShapeDtypeStruct((64, 1024),...  14 us
    pallas_call x1, Pallas kernels, final(): pl.pallas_call(final_kernel, out_shape=jax.ShapeDtypeStruct((128, 8, 64),...  2.11 us

commit v1 on v0

--- a/solution.py
+++ b/solution.py
@@ -49,8 +49,8 @@
 
 
 def halo_kernel(
-    points_ref, near_ref, counts_ref, table_ref, slots_ref, blocks_ref, info_ref, rank_ref,
-    main, send, recv,
+    points_ref, near_any, counts_ref, table_ref, slots_ref, blocks_ref, info_ref, rank_ref,
+    main, near_ref, send, recv, loaded,
 ):
     me_x = lax.axis_index("gx")
     me_y = lax.axis_index("gy")
@@ -68,6 +68,8 @@
     peers = [o for o in OFFSETS if o != (0, 0, 0)]
     for offset in peers:
         pl.semaphore_signal(barrier, inc=1, device_id=device(offset), device_id_type=MESH)
+    load = pltpu.make_async_copy(near_any, near_ref, loaded)
+    load.start()
 
     main[13] = jnp.concatenate([points_ref[d] for d in range(6)] + [jnp.zeros((2, 512), F32)], axis=0).astype(BF16)
     pl.semaphore_wait(barrier, len(peers))
@@ -100,6 +102,7 @@
         )
         rank = rank + jnp.dot(ones, ahead, preferred_element_type=F32)
     rank_ref[...] = rank
+    load.wait()
     near = jnp.concatenate(
         [near_ref[pl.ds(z, 128, stride=8), :].astype(F32).T for z in range(8)], axis=1
     ).astype(jnp.int32)
@@ -144,12 +147,14 @@
             jax.ShapeDtypeStruct((8, 8, 128), F32),
             jax.ShapeDtypeStruct((8, 1024), F32),
         ],
-        in_specs=[vmem] * 3,
+        in_specs=[vmem, pl.BlockSpec(memory_space=pl.ANY), vmem],
         out_specs=[vmem] * 5,
         scratch_shapes=[
             pltpu.VMEM((27, 8, 512), BF16),
+            pltpu.VMEM((1024, NB), jnp.int32),
             pltpu.SemaphoreType.DMA((1,)),
             pltpu.SemaphoreType.DMA((1,)),
+            pltpu.SemaphoreType.DMA,
         ],
         compiler_params=pltpu.CompilerParams(collective_id=1, has_side_effects=True),
     )(points, near, counts)
@@ -344,9 +349,9 @@
 
 
 def spectral_kernel(
-    ordered_ref, rank_ref, skip_ref, weight_any, third_any, back_any, second_any, first_any, firstt_any, pair_any,
+    ordered_any, rank_any, skip_ref, weight_any, third_any, back_any, second_any, first_any, firstt_any, pair_any,
     out_ref,
-    weight_ref, third_ref, back_ref, second_ref, first_ref, firstt_ref, pair_ref,
+    weight_ref, third_ref, back_ref, second_ref, first_ref, firstt_ref, pair_ref, ordered_ref, rank_ref,
     latent, l_msg, r1, w_msg, rw, s_msg, r3, mixing, mixed_scr, n_msg, r5, g_msg, r6, b_msg, r8, ended, skip,
     send, recv, loaded,
 ):
@@ -373,8 +378,14 @@
     constants = (weight_any, third_any, back_any, second_any, first_any, firstt_any, pair_any)
     copies = (weight_ref, third_ref, back_ref, second_ref, first_ref, firstt_ref, pair_ref)
     loads = [pltpu.make_async_copy(c, d, loaded.at[n]) for n, (c, d) in enumerate(zip(constants, copies))]
-    for load in loads:
+    early = [
+        pltpu.make_async_copy(c, d, loaded.at[7 + n])
+        for n, (c, d) in enumerate(((ordered_any, ordered_ref), (rank_any, rank_ref)))
+    ]
+    for load in early + loads:
         load.start()
+    for load in early:
+        load.wait()
     order = lax.broadcasted_iota(jnp.int32, (1024, 128), 0).astype(F32)
     for z in range(8):
         moved = jnp.where(order == rank_ref[0:1, 128 * z : 128 * z + 128], 1.0, 0.0).astype(BF16)
@@ -563,11 +574,11 @@
 
 def spectral_layer(ordered, rank, skip_w, weight, *tables):
     vmem = pl.BlockSpec(memory_space=pltpu.VMEM)
-    own = [pltpu.VMEM(array.shape, array.dtype) for array in (weight,) + tables]
+    own = [pltpu.VMEM(array.shape, array.dtype) for array in (weight,) + tables + (ordered, rank)]
     return pl.pallas_call(
         spectral_kernel,
         out_shape=jax.ShapeDtypeStruct((8, 64, 128), F32),
-        in_specs=[vmem] * 3 + [pl.BlockSpec(memory_space=pl.ANY)] * 7,
+        in_specs=[pl.BlockSpec(memory_space=pl.ANY)] * 2 + [vmem] + [pl.BlockSpec(memory_space=pl.ANY)] * 7,
         out_specs=vmem,
         scratch_shapes=own
         + [
@@ -590,7 +601,7 @@
             pltpu.VMEM((8, 64, 128), F32),
             pltpu.SemaphoreType.DMA((6,)),
             pltpu.SemaphoreType.DMA((6,)),
-            pltpu.SemaphoreType.DMA((7,)),
+            pltpu.SemaphoreType.DMA((9,)),
         ],
         compiler_params=pltpu.CompilerParams(collective_id=0, has_side_effects=True),
     )(ordered, rank, skip_w, weight, *tables)

time: 66.9 us -> 66.3 us (level); the launches traced: 66.9 us -> 65.6 us
  Pallas kernels: 66.9 us -> 65.6 us
    pallas_call x1, Pallas kernels: 34.6 us -> 33 us  [spectral_layer(): pl.pallas_call(spectral_kernel, out_shape=jax.ShapeDtypeStruct((8, 64, 12...]
where the time goes in v1:
time: 66.3 us; the launch traced here: 65.6 us
  Pallas kernels  65.6 us (99%)
    pallas_call x1, Pallas kernels, spectral_layer(): pl.pallas_call(spectral_kernel, out_shape=jax.ShapeDtypeStruct((8, 64, 12...  33 us
    pallas_call x1, Pallas kernels, halo(): pl.pallas_call(halo_kernel, out_shape=[jax.ShapeDtypeStruct((2 * ROWS, 25...  15.9 us
    pallas_call x1, Pallas kernels, encode(): pl.pallas_call(encoder_kernel, out_shape=jax.ShapeDtypeStruct((64, 1024),...  14.6 us
    pallas_call x1, Pallas kernels, final(): pl.pallas_call(final_kernel, out_shape=jax.ShapeDtypeStruct((128, 8, 64),...  2.11 us

profile of v1, /device:TPU:1, one launch (start us, length us, event | category | flops | bytes accessed | tf_op | source)
XLA Modules:
  0.0 65.6 jit_solution(9649344396913022349)
XLA Ops:
  0.0 15.9 %shard_map.136 = (bf16[352,256]{1,0:T(8,128)(2,1)}, s32[8,32,128]{2,1,0:T(8,128)}, s32[8,32,128]{2,1,0:T(8,128)}, f32[8,8,128]{2,1,0:T(8,128)}, f32[8,1024]{1,0:T(8,128)}) custom-call(f32[6,1,512]{2,1,0:T(1,128)} %bitcast.12, s32[1024,32]{1,0:T(8,128)} %bitcast.9, s32[8,8,16]{2,1,0:T(8,128)} %bitcast.10), custom_call_target="tpu_custom_call" | custom-call | tf_op jit(solution)/shard_map/pallas_call | solution.py:141
  15.9 14.6 %shard_map.137.ordered_any = bf16[64,1024]{1,0:T(8,128)(2,1)} custom-call(bf16[352,256]{1,0:T(8,128)(2,1)} %get-tuple-element.10.table_ref, s32[8,32,128]{2,1,0:T(8,128)} %get-tuple-element.11.slots_ref, s32[8,32,128]{2,1,0:T(8,128)} %get-tuple-element.12.blocks_ref, f32[8,8,128]{2,1,0:T(8,128)} %get-tuple-element.13.info_ref, bf16[6,80]{1,0:T(8,128)(2,1)} %in_ref.1, ...), custom_call_target="tpu_custom_call" | custom-call | tf_op jit(solution)/shard_map/pallas_call | solution.py:255
  30.5 33.0 %shard_map.138.cells_ref = f32[8,64,128]{2,1,0:T(8,128)} custom-call(bf16[64,1024]{1,0:T(8,128)(2,1)} %shard_map.137.ordered_any, f32[8,1024]{1,0:T(8,128)} %get-tuple-element.14.rank_any, bf16[64,64]{1,0:T(8,128)(2,1)} %skip_ref.1, bf16[2,16,64,64]{3,2,1,0:T(8,128)(2,1)} %bitcast.8, bf16[2,64,128]{2,1,0:T(8,128)(2,1)} %constant.12.clone.third_any, ...), custom_call_target="tpu_custom_call" | custom-call | tf_op jit(solution)/shard_map/pallas_call | solution.py:578
  63.5 2.1 %shard_map.139 = f32[128,8,64]{2,1,0:T(8,128)} custom-call(f32[8,64,128]{2,1,0:T(8,128)} %shard_map.138.cells_ref), custom_call_target="tpu_custom_call" | custom-call | tf_op jit(solution)/shard_map/pallas_call | solution.py:570

commit v2 on v0

--- a/solution.py
+++ b/solution.py
@@ -11,6 +11,7 @@
 from jax.sharding import PartitionSpec as P
 
 GRID = 64
+LIMIT = 24 * 2**20
 MODES = 16
 NB = 32
 NORM_FLOOR = 1.0
@@ -39,6 +40,14 @@
 FOUR, SIX = 108, 162
 GELU16 = True
 OFFSETS = [(dx, dy, dz) for dx in (-1, 0, 1) for dy in (-1, 0, 1) for dz in (-1, 0, 1)]
+
+
+def kept(*arrays):
+    return [pltpu.with_memory_space_constraint(array, pltpu.VMEM) for array in arrays]
+
+
+def far(*arrays):
+    return [pltpu.with_memory_space_constraint(array, pltpu.HBM) for array in arrays]
 
 
 def regroup():
@@ -138,11 +147,11 @@
     return pl.pallas_call(
         halo_kernel,
         out_shape=[
-            jax.ShapeDtypeStruct((2 * ROWS, 256), BF16),
-            jax.ShapeDtypeStruct((8, NB, 128), jnp.int32),
-            jax.ShapeDtypeStruct((8, NB, 128), jnp.int32),
-            jax.ShapeDtypeStruct((8, 8, 128), F32),
-            jax.ShapeDtypeStruct((8, 1024), F32),
+            pltpu.VMEM((2 * ROWS, 256), BF16),
+            pltpu.VMEM((8, NB, 128), jnp.int32),
+            pltpu.VMEM((8, NB, 128), jnp.int32),
+            pltpu.VMEM((8, 8, 128), F32),
+            pltpu.VMEM((8, 1024), F32),
         ],
         in_specs=[vmem] * 3,
         out_specs=[vmem] * 5,
@@ -151,8 +160,8 @@
             pltpu.SemaphoreType.DMA((1,)),
             pltpu.SemaphoreType.DMA((1,)),
         ],
-        compiler_params=pltpu.CompilerParams(collective_id=1, has_side_effects=True),
-    )(points, near, counts)
+        compiler_params=pltpu.CompilerParams(collective_id=1, has_side_effects=True, vmem_limit_bytes=LIMIT),
+    )(*far(points, near, counts))
 
 
 def encoder_kernel(
@@ -249,7 +258,7 @@
     vmem = pl.BlockSpec(memory_space=pltpu.VMEM)
     return pl.pallas_call(
         encoder_kernel,
-        out_shape=jax.ShapeDtypeStruct((64, 1024), BF16),
+        out_shape=pltpu.VMEM((64, 1024), BF16),
         in_specs=[vmem] * 7,
         out_specs=vmem,
         scratch_shapes=[
@@ -262,7 +271,8 @@
             pltpu.VMEM((9, 80, 128), F32),
             pltpu.SMEM((8,), jnp.int32),
         ],
-    )(table, slots, blocks, info, kernel_in, kernel_mid, kernel_out)
+        compiler_params=pltpu.CompilerParams(vmem_limit_bytes=LIMIT),
+    )(*kept(table, slots, blocks, info), *far(kernel_in, kernel_mid, kernel_out))
 
 
 def halves(values):
@@ -557,8 +567,9 @@
 def final(cells):
     vmem = pl.BlockSpec(memory_space=pltpu.VMEM)
     return pl.pallas_call(
-        final_kernel, out_shape=jax.ShapeDtypeStruct((128, 8, 64), F32), in_specs=[vmem], out_specs=vmem
-    )(cells)
+        final_kernel, out_shape=jax.ShapeDtypeStruct((128, 8, 64), F32), in_specs=[vmem], out_specs=vmem,
+        compiler_params=pltpu.CompilerParams(vmem_limit_bytes=LIMIT),
+    )(*kept(cells))
 
 
 def spectral_layer(ordered, rank, skip_w, weight, *tables):
@@ -566,8 +577,8 @@
     own = [pltpu.VMEM(array.shape, array.dtype) for array in (weight,) + tables]
     return pl.pallas_call(
         spectral_kernel,
-        out_shape=jax.ShapeDtypeStruct((8, 64, 128), F32),
-        in_specs=[vmem] * 3 + [pl.BlockSpec(memory_space=pl.ANY)] * 7,
+        out_shape=pltpu.VMEM((8, 64, 128), F32),
+        in_specs=[vmem] * 3 + [pl.BlockSpec(memory_space=pltpu.HBM)] * 7,
         out_specs=vmem,
         scratch_shapes=own
         + [
@@ -592,8 +603,8 @@
             pltpu.SemaphoreType.DMA((6,)),
             pltpu.SemaphoreType.DMA((7,)),
         ],
-        compiler_params=pltpu.CompilerParams(collective_id=0, has_side_effects=True),
-    )(ordered, rank, skip_w, weight, *tables)
+        compiler_params=pltpu.CompilerParams(collective_id=0, has_side_effects=True, vmem_limit_bytes=LIMIT),
+    )(*kept(ordered, rank), *far(skip_w, weight, *tables))
 
 
 def body(point_data, neighbours, counts, kernel_in, kernel_mid, kernel_out, spectral, skip_weight):

time: 66.9 us -> 63.4 us (0.948)
  Pallas kernels: 66.9 us -> 63.2 us
    pallas_call x3, Pallas kernels: 64.8 us -> 62.1 us  [the longest x1 31.9 us: spectral_layer(): pl.pallas_call(spectral_kernel, out_shape=pltpu.VMEM((8, 64, 128), F32),...]
    pallas_call x1, Pallas kernels: 2.11 us -> 1.17 us  [final(): pl.pallas_call(final_kernel, out_shape=jax.ShapeDtypeStruct((128, 8, 64),...]
where the time goes in v2:
time: 63.4 us; the launch traced here: 63.3 us
  Pallas kernels  63.2 us (100%)
    pallas_call x1, Pallas kernels, spectral_layer(): pl.pallas_call(spectral_kernel, out_shape=pltpu.VMEM((8, 64, 128), F32),...  31.9 us
    pallas_call x1, Pallas kernels, halo(): pl.pallas_call(halo_kernel, out_shape=[pltpu.VMEM((2 * ROWS, 256), BF16),...  15.4 us
    pallas_call x1, Pallas kernels, encode(): pl.pallas_call(encoder_kernel, out_shape=pltpu.VMEM((64, 1024), BF16), in...  14.8 us

profile of v2, /device:TPU:1, one launch (start us, length us, event | category | flops | bytes accessed | tf_op | source)
XLA Modules:
  0.0 63.3 jit_solution(13339578408401582250)
XLA Ops:
  0.0 15.4 %shard_map.136 = (bf16[352,256]{1,0:T(8,128)(2,1)S(1)}, s32[8,32,128]{2,1,0:T(8,128)S(1)}, s32[8,32,128]{2,1,0:T(8,128)S(1)}, f32[8,8,128]{2,1,0:T(8,128)S(1)}, f32[8,1024]{1,0:T(8,128)S(1)}) custom-call(f32[6,1,512]{2,1,0:T(1,128)} %bitcast.12, s32[1024,32]{1,0:T(8,128)} %bitcast.9, s32[8,8,16]{2,1,0:T(8,128)} %bitcast.10), custom_call_target="tpu_custom_call" | custom-call | tf_op jit(solution)/shard_map/pallas_call | solution.py:147
  15.4 14.8 %shard_map.137.ordered_ref = bf16[64,1024]{1,0:T(8,128)(2,1)S(1)} custom-call(bf16[352,256]{1,0:T(8,128)(2,1)S(1)} %get-tuple-element.10.table_ref, s32[8,32,128]{2,1,0:T(8,128)S(1)} %get-tuple-element.11.slots_ref, s32[8,32,128]{2,1,0:T(8,128)S(1)} %get-tuple-element.12.blocks_ref, f32[8,8,128]{2,1,0:T(8,128)S(1)} %get-tuple-element.13.info_ref, ...), custom_call_target="tpu_custom_call" | custom-call | tf_op jit(solution)/shard_map/pallas_call | solution.py:259
  30.2 31.9 %shard_map.138.cells_ref = f32[8,64,128]{2,1,0:T(8,128)S(1)} custom-call(bf16[64,1024]{1,0:T(8,128)(2,1)S(1)} %shard_map.137.ordered_ref, f32[8,1024]{1,0:T(8,128)S(1)} %get-tuple-element.14.rank_ref, bf16[64,64]{1,0:T(8,128)(2,1)} %skip_ref.1, bf16[2,16,64,64]{3,2,1,0:T(8,128)(2,1)} %bitcast.8, bf16[2,64,128]{2,1,0:T(8,128)(2,1)} %constant.12.clone.third_any, ...), custom_call_target="tpu_custom_call" | custom-call | tf_op jit(solution)/shard_map/pallas_call | solution.py:578
  62.1 1.2 %shard_map.139 = f32[128,8,64]{2,1,0:T(8,128)} custom-call(f32[8,64,128]{2,1,0:T(8,128)S(1)} %shard_map.138.cells_ref), custom_call_target="tpu_custom_call" | custom-call | tf_op jit(solution)/shard_map/pallas_call | solution.py:569

commit v3 on v2

--- a/solution.py
+++ b/solution.py
@@ -58,8 +58,9 @@
 
 
 def halo_kernel(
-    points_ref, near_ref, counts_ref, table_ref, slots_ref, blocks_ref, info_ref, rank_ref,
-    main, send, recv,
+    points_any, near_any, counts_any, in_any, mid_any, last_any, skip_any,
+    table_ref, slots_ref, blocks_ref, info_ref, rank_ref, first_out, mid_out, last_out, skip_out,
+    points_ref, near_ref, counts_ref, in_ref, mid_ref, skip_ref, main, send, recv, loaded,
 ):
     me_x = lax.axis_index("gx")
     me_y = lax.axis_index("gy")
@@ -77,6 +78,14 @@
     peers = [o for o in OFFSETS if o != (0, 0, 0)]
     for offset in peers:
         pl.semaphore_signal(barrier, inc=1, device_id=device(offset), device_id_type=MESH)
+    moves = (
+        (points_any, points_ref), (counts_any, counts_ref), (near_any, near_ref), (in_any, in_ref),
+        (mid_any, mid_ref), (last_any, last_out), (skip_any, skip_ref),
+    )
+    loads = [pltpu.make_async_copy(c, d, loaded.at[n]) for n, (c, d) in enumerate(moves)]
+    for load in loads:
+        load.start()
+    loads[0].wait()
 
     main[13] = jnp.concatenate([points_ref[d] for d in range(6)] + [jnp.zeros((2, 512), F32)], axis=0).astype(BF16)
     pl.semaphore_wait(barrier, len(peers))
@@ -92,6 +101,8 @@
         ).start()
     everything = main.at[pl.ds(0, 26)]
 
+    for load in loads[1:]:
+        load.wait()
     lane = lax.broadcasted_iota(jnp.int32, (1, 1024), 1)
     counts = jnp.concatenate([counts_ref[x].astype(F32) for x in range(8)], axis=1)
     counts = jnp.concatenate([counts[z : z + 1] for z in range(8)], axis=1)
@@ -132,6 +143,20 @@
         blocks_ref[t] = moved[32:64].astype(jnp.int32)
         info_ref[t] = moved[64:72]
 
+    column = lax.broadcasted_iota(jnp.int32, (6, ROWS), 1)
+    feature = lax.broadcasted_iota(jnp.int32, (6, ROWS), 0)
+    wanted = jnp.where(column < FOUR, column % 4, 4 + column % 2)
+    wanted = jnp.where(column >= SIX, column - SIX, wanted)
+    chosen = jnp.where((feature == wanted) & (column < SIX + 3), 1.0, 0.0).astype(BF16)
+    turn = (((0,), (0,)), ((), ()))
+    first_out[...] = lax.dot_general(in_ref[...], chosen, turn, preferred_element_type=F32).astype(BF16)
+    half_mid = (mid_ref[...].astype(F32).T * 0.5).astype(BF16)
+    mid_out[...] = jnp.zeros(mid_out.shape, BF16)
+    mid_out[0:80, 0:80] = half_mid
+    mid_out[80:160, 80:160] = half_mid
+
+    skip_out[...] = skip_ref[...].astype(F32).T.astype(BF16)
+
     pltpu.make_async_copy(everything, everything, recv.at[0]).wait()
     blocks = [main[b].astype(F32) for b in range(27)]
     rows = [block[0:4] for block in blocks] + [block[4:6] for block in blocks]
@@ -142,7 +167,7 @@
     pltpu.make_async_copy(everything, everything, send.at[0]).wait()
 
 
-def halo(points, near, counts):
+def halo(points, near, counts, kernel_in, kernel_mid, last, skip_w):
     vmem = pl.BlockSpec(memory_space=pltpu.VMEM)
     return pl.pallas_call(
         halo_kernel,
@@ -152,35 +177,33 @@
             pltpu.VMEM((8, NB, 128), jnp.int32),
             pltpu.VMEM((8, 8, 128), F32),
             pltpu.VMEM((8, 1024), F32),
+            pltpu.VMEM((80, ROWS), BF16),
+            pltpu.VMEM((160, 160), BF16),
+            pltpu.VMEM((64, 80), BF16),
+            pltpu.VMEM((64, 64), BF16),
         ],
-        in_specs=[vmem] * 3,
-        out_specs=[vmem] * 5,
+        in_specs=[pl.BlockSpec(memory_space=pl.ANY)] * 7,
+        out_specs=[vmem] * 9,
         scratch_shapes=[
+            pltpu.VMEM(points.shape, F32),
+            pltpu.VMEM(near.shape, jnp.int32),
+            pltpu.VMEM(counts.shape, jnp.int32),
+            pltpu.VMEM(kernel_in.shape, BF16),
+            pltpu.VMEM(kernel_mid.shape, BF16),
+            pltpu.VMEM(skip_w.shape, BF16),
             pltpu.VMEM((27, 8, 512), BF16),
             pltpu.SemaphoreType.DMA((1,)),
             pltpu.SemaphoreType.DMA((1,)),
+            pltpu.SemaphoreType.DMA((7,)),
         ],
         compiler_params=pltpu.CompilerParams(collective_id=1, has_side_effects=True, vmem_limit_bytes=LIMIT),
-    )(*far(points, near, counts))
+    )(*far(points, near, counts, kernel_in, kernel_mid, last, skip_w))
 
 
 def encoder_kernel(
-    table_ref, slots_ref, blocks_ref, info_ref, in_ref, mid_ref, last_ref, out_ref,
-    first_scr, mid_scr, last_scr, kept_scr, hidden_scr, base_scr, totals, trips,
+    table_ref, slots_ref, blocks_ref, info_ref, first_scr, mid_scr, last_scr, out_ref,
+    kept_scr, hidden_scr, base_scr, totals, trips,
 ):
-    column = lax.broadcasted_iota(jnp.int32, (6, ROWS), 1)
-    feature = lax.broadcasted_iota(jnp.int32, (6, ROWS), 0)
-    wanted = jnp.where(column < FOUR, column % 4, 4 + column % 2)
-    wanted = jnp.where(column >= SIX, column - SIX, wanted)
-    chosen = jnp.where((feature == wanted) & (column < SIX + 3), 1.0, 0.0).astype(BF16)
-    turn = (((0,), (0,)), ((), ()))
-    first_scr[...] = lax.dot_general(in_ref[...], chosen, turn, preferred_element_type=F32).astype(BF16)
-    half_mid = (mid_ref[...].astype(F32).T * 0.5).astype(BF16)
-    mid_scr[...] = jnp.zeros(mid_scr.shape, BF16)
-    mid_scr[0:80, 0:80] = half_mid
-    mid_scr[80:160, 80:160] = half_mid
-    last_scr[...] = last_ref[...]
-
     slot_ids = lax.broadcasted_iota(jnp.int32, (256, 128), 0).astype(jnp.int16)
     row = lax.broadcasted_iota(jnp.int32, (ROWS, 128), 0)
     row_block = jnp.where(row < FOUR, row // 4, jnp.where(row < SIX, (row - FOUR) // 2, -1)).astype(jnp.int16)
@@ -254,7 +277,7 @@
     out_ref[...] = jnp.concatenate(ordered, axis=1)
 
 
-def encode(table, slots, blocks, info, kernel_in, kernel_mid, kernel_out):
+def encode(*made):
     vmem = pl.BlockSpec(memory_space=pltpu.VMEM)
     return pl.pallas_call(
         encoder_kernel,
@@ -262,9 +285,6 @@
         in_specs=[vmem] * 7,
         out_specs=vmem,
         scratch_shapes=[
-            pltpu.VMEM((80, ROWS), BF16),
-            pltpu.VMEM((160, 160), BF16),
-            pltpu.VMEM((64, 80), BF16),
             pltpu.VMEM((ROWS, 128 * SLOTS), BF16),
             pltpu.VMEM((160, 256), BF16),
             pltpu.VMEM((8, 16, 128), BF16),
@@ -272,7 +292,7 @@
             pltpu.SMEM((8,), jnp.int32),
         ],
         compiler_params=pltpu.CompilerParams(vmem_limit_bytes=LIMIT),
-    )(*kept(table, slots, blocks, info), *far(kernel_in, kernel_mid, kernel_out))
+    )(*kept(*made))
 
 
 def halves(values):
@@ -437,9 +457,8 @@
         load.wait()
     first_tab = [[spread_blocks(first_ref, p, l) for l in range(2)] for p in range(2)]
     back_tab = [[spread_blocks(firstt_ref, p, l) for l in range(2)] for p in range(2)]
-    skip_t = skip_ref[...].astype(F32).T.astype(BF16)
     for z in range(8):
-        skip[z] = dotf(skip_t, latent[64 * z : 64 * z + 64].astype(BF16))
+        skip[z] = dotf(skip_ref[...], latent[64 * z : 64 * z + 64].astype(BF16))
     finish(first)
 
     pieces = []
@@ -572,7 +591,7 @@
     )(*kept(cells))
 
 
-def spectral_layer(ordered, rank, skip_w, weight, *tables):
+def spectral_layer(ordered, rank, skip_t, weight, *tables):
     vmem = pl.BlockSpec(memory_space=pltpu.VMEM)
     own = [pltpu.VMEM(array.shape, array.dtype) for array in (weight,) + tables]
     return pl.pallas_call(
@@ -604,23 +623,27 @@
             pltpu.SemaphoreType.DMA((7,)),
         ],
         compiler_params=pltpu.CompilerParams(collective_id=0, has_side_effects=True, vmem_limit_bytes=LIMIT),
-    )(*kept(ordered, rank), *far(skip_w, weight, *tables))
+    )(*kept(ordered, rank, skip_t), *far(weight, *tables))
 
 
 def body(point_data, neighbours, counts, kernel_in, kernel_mid, kernel_out, spectral, skip_weight):
     cells_x, cells_y, cells_z = neighbours.shape[1:4]
-    made = halo(
+    *made, rank, first, mid, last, skip_t = halo(
         jnp.transpose(point_data, (1, 0, 2)),
         neighbours.reshape(-1, NB),
         jnp.transpose(counts[0], (0, 2, 1)),
-    )
-    ordered = encode(*made[:4], kernel_in, kernel_mid, kernel_out.T)
+        kernel_in,
+        kernel_mid,
+        kernel_out.T,
+        skip_weight,
+    )
+    ordered = encode(*made, first, mid, last)
     third = third_table()
     by_place = first_table()
     cells = spectral_layer(
         ordered,
-        made[4],
-        skip_weight,
+        rank,
+        skip_t,
         spectral.reshape(2, 16, 64, 64),
         jnp.asarray(halves(third)),
         jnp.asarray(halves(third.T)),

time: 63.4 us -> 61.1 us (0.964)
  Pallas kernels: 63.2 us -> 60.9 us
    pallas_call x1, Pallas kernels: 14.8 us -> 12.8 us  [encode(): pl.pallas_call(encoder_kernel, out_shape=pltpu.VMEM((64, 1024), BF16), in...]
    pallas_call x1, Pallas kernels: 15.4 us -> 14.4 us  [halo(): pl.pallas_call(halo_kernel, out_shape=[pltpu.VMEM((2 * ROWS, 256), BF16),...]
    pallas_call x1, Pallas kernels: 31.9 us -> 32.6 us  [spectral_layer(): pl.pallas_call(spectral_kernel, out_shape=pltpu.VMEM((8, 64, 128), F32),...]
where the time goes in v3:
time: 61.1 us; the launch traced here: 61 us
  Pallas kernels  60.9 us (100%)
    pallas_call x1, Pallas kernels, spectral_layer(): pl.pallas_call(spectral_kernel, out_shape=pltpu.VMEM((8, 64, 128), F32),...  32.6 us
    pallas_call x1, Pallas kernels, halo(): pl.pallas_call(halo_kernel, out_shape=[pltpu.VMEM((2 * ROWS, 256), BF16),...  14.4 us
    pallas_call x1, Pallas kernels, encode(): pl.pallas_call(encoder_kernel, out_shape=pltpu.VMEM((64, 1024), BF16), in...  12.8 us

profile of v3, /device:TPU:1, one launch (start us, length us, event | category | flops | bytes accessed | tf_op | source)
XLA Modules:
  0.0 61.0 jit_solution(14128601500144202486)
XLA Ops:
  0.0 14.4 %shard_map.136 = (bf16[352,256]{1,0:T(8,128)(2,1)S(1)}, s32[8,32,128]{2,1,0:T(8,128)S(1)}, s32[8,32,128]{2,1,0:T(8,128)S(1)}, f32[8,8,128]{2,1,0:T(8,128)S(1)}, ...) custom-call(f32[6,1,512]{2,1,0:T(1,128)} %bitcast.12, ...), custom_call_target="tpu_custom_call" | custom-call | tf_op jit(solution)/shard_map/pallas_call | solution.py:172
  14.4 12.8 %shard_map.137.ordered_ref = bf16[64,1024]{1,0:T(8,128)(2,1)S(1)} custom-call(bf16[352,256]{1,0:T(8,128)(2,1)S(1)} %get-tuple-element.14.table_ref, s32[8,32,128]{2,1,0:T(8,128)S(1)} %get-tuple-element.15.slots_ref, s32[8,32,128]{2,1,0:T(8,128)S(1)} %get-tuple-element.16.blocks_ref, f32[8,8,128]{2,1,0:T(8,128)S(1)} %get-tuple-element.17.info_ref, ...), custom_call_target="tpu_custom_call" | custom-call | tf_op jit(solution)/shard_map/pallas_call | solution.py:282
  27.2 32.6 %shard_map.138.cells_ref = f32[8,64,128]{2,1,0:T(8,128)S(1)} custom-call(bf16[64,1024]{1,0:T(8,128)(2,1)S(1)} %shard_map.137.ordered_ref, f32[8,1024]{1,0:T(8,128)S(1)} %get-tuple-element.21.rank_ref, bf16[64,64]{1,0:T(8,128)(2,1)S(1)} %get-tuple-element.22.skip_ref, bf16[2,16,64,64]{3,2,1,0:T(8,128)(2,1)} %bitcast.8, ...), custom_call_target="tpu_custom_call" | custom-call | tf_op jit(solution)/shard_map/pallas_call | solution.py:597
  59.8 1.2 %shard_map.139 = f32[128,8,64]{2,1,0:T(8,128)} custom-call(f32[8,64,128]{2,1,0:T(8,128)S(1)} %shard_map.138.cells_ref), custom_call_target="tpu_custom_call" | custom-call | tf_op jit(solution)/shard_map/pallas_call | solution.py:588

commit v4 on v3

--- a/solution.py
+++ b/solution.py
@@ -555,11 +555,9 @@
     low = (lanes128 // 2) % 16 == 0
     power = jnp.where(low, 0.5 * wide_field * (wide_field + paired), 2.0 * wide_field * wide_field)
     power = jnp.sum(power, axis=0, keepdims=True)
-    for shift in (64, 32, 16, 8, 4, 2):
-        power = power + pltpu.roll(power, shift, 1)
-    lane = lax.broadcasted_iota(jnp.int32, (1, 128), 1)
-    power = jnp.where(lane % 2 == (lane // 8) % 2, power, pltpu.roll(power, 1, 1))
-    variance = jnp.broadcast_to(power, (128, 128)).T * (scale * scale)
+    chosen = jnp.where(lanes128 % 2 == (rows128 // 8) % 2, 1.0, 0.0).astype(BF16)
+    high, low_part = split(jnp.broadcast_to(power, (128, 128)))
+    variance = (dott(chosen, high) + dott(chosen, low_part)) * (scale * scale)
     inverse = 1.0 / jnp.sqrt(variance + NORM_FLOOR)
     for e in range(4):
         part = jnp.concatenate(

time: 61.1 us -> 61.2 us (level)
  no operation moved by 1% of the time
where the time goes in v4:
time: 61.2 us
  Pallas kernels  61.2 us (100%)
    pallas_call x1, Pallas kernels, spectral_layer(): pl.pallas_call(spectral_kernel, out_shape=pltpu.VMEM((8, 64, 128), F32),...  32.8 us
    pallas_call x1, Pallas kernels, halo(): pl.pallas_call(halo_kernel, out_shape=[pltpu.VMEM((2 * ROWS, 256), BF16),...  14.4 us
    pallas_call x1, Pallas kernels, encode(): pl.pallas_call(encoder_kernel, out_shape=pltpu.VMEM((64, 1024), BF16), in...  12.8 us

profile of v4, /device:TPU:1, one launch (start us, length us, event | category | flops | bytes accessed | tf_op | source)
XLA Modules:
  0.0 61.2 jit_solution(12931992483703867258)
XLA Ops:
  0.0 14.4 %shard_map.136 = (bf16[352,256]{1,0:T(8,128)(2,1)S(1)}, s32[8,32,128]{2,1,0:T(8,128)S(1)}, s32[8,32,128]{2,1,0:T(8,128)S(1)}, f32[8,8,128]{2,1,0:T(8,128)S(1)}, ...) custom-call(f32[6,1,512]{2,1,0:T(1,128)} %bitcast.12, ...), custom_call_target="tpu_custom_call" | custom-call | tf_op jit(solution)/shard_map/pallas_call | solution.py:172
  14.4 12.8 %shard_map.137.ordered_ref = bf16[64,1024]{1,0:T(8,128)(2,1)S(1)} custom-call(bf16[352,256]{1,0:T(8,128)(2,1)S(1)} %get-tuple-element.14.table_ref, s32[8,32,128]{2,1,0:T(8,128)S(1)} %get-tuple-element.15.slots_ref, s32[8,32,128]{2,1,0:T(8,128)S(1)} %get-tuple-element.16.blocks_ref, f32[8,8,128]{2,1,0:T(8,128)S(1)} %get-tuple-element.17.info_ref, ...), custom_call_target="tpu_custom_call" | custom-call | tf_op jit(solution)/shard_map/pallas_call | solution.py:282
  27.2 32.8 %shard_map.138.cells_ref = f32[8,64,128]{2,1,0:T(8,128)S(1)} custom-call(bf16[64,1024]{1,0:T(8,128)(2,1)S(1)} %shard_map.137.ordered_ref, f32[8,1024]{1,0:T(8,128)S(1)} %get-tuple-element.21.rank_ref, bf16[64,64]{1,0:T(8,128)(2,1)S(1)} %get-tuple-element.22.skip_ref, bf16[2,16,64,64]{3,2,1,0:T(8,128)(2,1)} %bitcast.8, ...), custom_call_target="tpu_custom_call" | custom-call | tf_op jit(solution)/shard_map/pallas_call | solution.py:595
  60.0 1.2 %shard_map.139 = f32[128,8,64]{2,1,0:T(8,128)} custom-call(f32[8,64,128]{2,1,0:T(8,128)S(1)} %shard_map.138.cells_ref), custom_call_target="tpu_custom_call" | custom-call | tf_op jit(solution)/shard_map/pallas_call | solution.py:586
